TPU v7x, 32 devices: a whole 2x2x4 slice. The times are simulated.
32 devices in a mesh: row: 4 (over y, x), col: 8 (over z, core).
Axes of the slice: x: 2, y: 2, z: 4, core: 2. Of those that a mesh axis runs over, the one named last changes fastest.
Arguments:
- out_grad: bfloat16 [4096, 512], P('col', 'row'), may hold values from -6 to 6
- node_in: bfloat16 [4096, 512], P(('row', 'col')), may hold values from -0.09375 to 0.09375
- weights: bfloat16 [3, 512, 512], replicated, may hold values from -0.25 to 0.25
- tile_vals: bfloat16 [3, 8, 4, 32, 128, 128], P(None, 'col', 'row'), may hold values from -0.15625 to 0.15625
- tile_rows: int32 [3, 8, 4, 32], P(None, 'col', 'row'), may hold values from 0 to 3
- tile_cols: int32 [3, 8, 4, 32], P(None, 'col', 'row'), may hold values from 0 to 7
- tile_count: int32 [3, 8, 4], P(None, 'col', 'row'), may hold values from 1 to 32, as said below
Outputs:
- d_nodes: bfloat16 [4096, 512], P(('row', 'col'))
- d_weights: float32 [3, 512, 512], replicated
Inputs may be any that keep to these rules, and one draw needn't show every extreme that they name: Only the first tile_count slots of a block's list hold tiles; later slots are ignored. In every relation some block uses all 32 slots. `tile_rows`: coordinates may repeat within a block's list; such tiles add.
All inputs are finite; a program needn't handle non-finite values.
Results may differ from a plain program's by a relative error of at most 0.005.
Values may be sent and summed in bfloat16 or wider, within the bound.
A program may use at most 256 MiB of HBM per device.

v0:
```python
import functools

import jax
import jax.numpy as jnp
from jax import lax
from jax.experimental import pallas as pl
from jax.experimental.pallas import tpu as pltpu
from jax.sharding import PartitionSpec as P

MESH = pl.DeviceIdType.MESH
F32 = jnp.float32
BF16 = jnp.bfloat16


def assemble_kernel(rows_ref, cols_ref, count_ref, tiles_ref, out_ref, total):
    relation = pl.program_id(0)
    tile_rows, tile_cols, tile = total.shape[0], total.shape[1], total.shape[2]
    for i in range(tile_rows):
        for j in range(tile_cols):
            total[i, j] = jnp.zeros((tile, tile), F32)

    def add_tile(slot, carry):
        i = rows_ref[relation, slot]
        j = cols_ref[relation, slot]
        total[i, j] = total[i, j] + tiles_ref[0, slot].astype(F32)
        return carry

    lax.fori_loop(0, count_ref[relation], add_tile, 0)
    for i in range(tile_rows):
        for j in range(tile_cols):
            out_ref[i * tile : (i + 1) * tile, j * tile : (j + 1) * tile] = total[i, j].astype(BF16)


def assemble(tile_vals, tile_rows, tile_cols, tile_count, targets, sources):
    relations, cap, tile = tile_vals.shape[0], tile_vals.shape[3], tile_vals.shape[4]
    vals = tile_vals.reshape(relations, cap, tile, tile)
    return pl.pallas_call(
        assemble_kernel,
        grid_spec=pltpu.PrefetchScalarGridSpec(
            num_scalar_prefetch=3,
            grid=(relations,),
            in_specs=[pl.BlockSpec((1, cap, tile, tile), lambda r, *_: (r, 0, 0, 0))],
            out_specs=pl.BlockSpec((targets, sources), lambda r, *_: (r, 0)),
            scratch_shapes=[pltpu.VMEM((targets // tile, sources // tile, tile, tile), F32)],
        ),
        out_shape=jax.ShapeDtypeStruct((relations * targets, sources), BF16),
        compiler_params=pltpu.CompilerParams(vmem_limit_bytes=60 * 2**20),
    )(
        tile_rows.reshape(relations, cap),
        tile_cols.reshape(relations, cap),
        tile_count.reshape(relations),
        vals,
    )


def main_kernel(
    nr, nc, relations,
    grad_ref, nodes_ref, w_hbm, a_hbm,
    dn_ref, ag_ref,
    gslot, g, w, a, xall, pt, nsend, nrecv, ncomb, ndst,
    dw, dwrecv, pbuf, precv, zbuf, zrecv,
    load_sem, gs, gr, xs, xr, fs, fr, ns, nrs, nzs, nzr, ds, dr, ps, pr, zs, zr,
    azs, azr, aps, apr, acs, acr,
):
    nz = nc // 2
    tn = grad_ref.shape[0]
    width = grad_ref.shape[1]
    nd = nodes_ref.shape[0]
    f = w_hbm.shape[1]
    me_r = lax.axis_index("row")
    me_c = lax.axis_index("col")
    z = me_c // 2
    core = me_c % 2
    other = 1 - core
    sibling = {"col": z * 2 + other}

    def row_peer(d):
        return {"row": lax.rem(me_r + d, nr)}

    def z_peer(d):
        return {"col": lax.rem(z + d, nz) * 2 + core}

    def remote(src, dst, send, recv, dev):
        return pltpu.make_async_remote_copy(
            src_ref=src, dst_ref=dst, send_sem=send, recv_sem=recv, device_id=dev, device_id_type=MESH
        )

    def x_slot(k):
        return xall.at[pl.ds(pl.multiple_of(k * nd, nd), nd), :]

    load_a = pltpu.make_async_copy(a_hbm, a, load_sem.at[0])
    load_w = pltpu.make_async_copy(w_hbm, w, load_sem.at[1])
    load_w.start()
    load_a.start()

    barrier = pltpu.get_barrier_semaphore()
    for d in range(1, nr):
        pl.semaphore_signal(barrier, inc=1, device_id=row_peer(d), device_id_type=MESH)
    for d in range(1, nz):
        pl.semaphore_signal(barrier, inc=1, device_id=z_peer(d), device_id_type=MESH)
    pl.semaphore_signal(barrier, inc=1, device_id=sibling, device_id_type=MESH)
    pl.semaphore_wait(barrier, nr - 1 + nz - 1 + 1)

    g_copies = [
        remote(grad_ref, gslot.at[me_r], gs.at[d - 1], gr.at[d - 1], row_peer(d)) for d in range(1, nr)
    ]
    for c in g_copies:
        c.start()
    x_copies = [
        remote(nodes_ref, x_slot(me_c), xs.at[d - 1], xr.at[d - 1], z_peer(d)) for d in range(1, nz)
    ]
    for c in x_copies:
        c.start()
    f_copies = [remote(nodes_ref, x_slot(me_c), fs.at[0], fr.at[0], sibling)]
    f_copies[0].start()
    xall[pl.ds(pl.multiple_of(me_c * nd, nd), nd), :] = nodes_ref[...]
    gslot[me_r] = grad_ref[...]

    load_w.wait()
    for c in g_copies:
        c.wait_recv()
    for k in range(nr):
        g[:, k * width : (k + 1) * width] = gslot[k]
    for r in range(relations):
        pt[:, r * tn : (r + 1) * tn] = lax.dot_general(
            w[r], g[...], (((1,), (1,)), ((), ())), preferred_element_type=F32
        ).astype(BF16)
    load_a.wait()

    def mix(k, carry):
        for h in range(2):
            cols = pl.ds(pl.multiple_of((k * 2 + h) * nd, nd), nd)
            nsend[h, k] = jnp.dot(pt[...], a[:, cols], preferred_element_type=F32)
        return carry

    lax.fori_loop(0, nz, mix, 0)
    n_core = remote(nsend.at[other], nrecv, ns.at[0], nrs.at[0], sibling)
    n_core.start()

    for d in range(1, nz):
        x_copies[d - 1].wait_recv()
        slot = lax.rem(z + nz - d, nz) * 2 + core
        c = remote(x_slot(slot), x_slot(slot), fs.at[d], fr.at[d], sibling)
        c.start()
        f_copies.append(c)

    n_core.wait_recv()

    def combine(k, carry):
        ncomb[k] = (nsend[core, k] + nrecv[k]).astype(BF16)
        return carry

    lax.fori_loop(0, nz, combine, 0)
    n_copies = []
    for d in range(1, nz):
        c = remote(ncomb.at[lax.rem(z + d, nz)], ndst.at[d - 1], nzs.at[d - 1], nzr.at[d - 1], z_peer(d))
        c.start()
        n_copies.append(c)

    for c in f_copies:
        c.wait_recv()

    chunk = f // 2
    for j in range(2 * relations):
        r, h = j // 2, j % 2
        y = jnp.dot(
            a[r * tn : (r + 1) * tn, :],
            xall[:, h * chunk : (h + 1) * chunk],
            preferred_element_type=F32,
        )
        yt = y.astype(BF16).T
        at = (j % relations) * chunk
        dw[j // relations, at : at + chunk, :] = jnp.dot(yt, g[...], preferred_element_type=F32)

    d_core = remote(dw.at[other], dwrecv, ds.at[0], dr.at[0], sibling)
    d_core.start()
    d_core.wait_recv()
    plane_rows = pbuf.shape[1]
    for k in range(nr):
        rows = slice(k * plane_rows, (k + 1) * plane_rows)
        pbuf[k] = (dw[core, rows, :] + dwrecv[rows, :]).astype(BF16)
    p_copies = []
    for d in range(1, nr):
        c = remote(pbuf.at[lax.rem(me_r + d, nr)], precv.at[d - 1], ps.at[d - 1], pr.at[d - 1], row_peer(d))
        c.start()
        p_copies.append(c)

    for c in n_copies:
        c.wait_recv()
    own = nsend[core, z] + nrecv[z]
    for d in range(1, nz):
        own = own + ndst[d - 1].astype(F32)
    dn_ref[...] = own.T.astype(BF16)

    for c in p_copies:
        c.wait_recv()
    piece = zbuf.shape[1]
    for k in range(nz):
        rows = slice(k * piece, (k + 1) * piece)
        part = pbuf[me_r, rows, :].astype(F32)
        for d in range(1, nr):
            part = part + precv[d - 1, rows, :].astype(F32)
        zbuf[k] = part
    z_copies = []
    for d in range(1, nz):
        c = remote(zbuf.at[lax.rem(z + d, nz)], zrecv.at[d - 1], zs.at[d - 1], zr.at[d - 1], z_peer(d))
        c.start()
        z_copies.append(c)
    for c in z_copies:
        c.wait_recv()
    final = zbuf[z]
    for d in range(1, nz):
        final = final + zrecv[d - 1]
    ag_ref[core, me_r, z] = final.astype(BF16)

    tail = []
    mine = ag_ref.at[core, me_r, z]
    az = [remote(mine, mine, azs.at[d - 1], azr.at[d - 1], z_peer(d)) for d in range(1, nz)]
    for c in az:
        c.start()
    for c in az:
        c.wait_recv()
    mine = ag_ref.at[core, me_r]
    ap = [remote(mine, mine, aps.at[d - 1], apr.at[d - 1], row_peer(d)) for d in range(1, nr)]
    for c in ap:
        c.start()
    ac = [remote(mine, mine, acs.at[0], acr.at[0], sibling)]
    ac[0].start()
    for d in range(1, nr):
        ap[d - 1].wait_recv()
        slot = ag_ref.at[core, lax.rem(me_r + nr - d, nr)]
        c = remote(slot, slot, acs.at[d], acr.at[d], sibling)
        c.start()
        ac.append(c)
    for c in ac:
        c.wait_recv()
    for c in g_copies + x_copies + f_copies + [n_core] + n_copies + [d_core] + p_copies + z_copies + az + ap + ac:
        c.wait_send()


def body(nr, nc, out_grad, node_in, weights, tile_vals, tile_rows, tile_cols, tile_count):
    relations, f = weights.shape[0], weights.shape[1]
    tn, width = out_grad.shape
    nd = node_in.shape[0]
    sn = nd * nc
    nz = nc // 2
    half = relations * f // 2
    plane_rows = half // nr
    piece = plane_rows // nz
    dense = assemble(tile_vals, tile_rows, tile_cols, tile_count, tn, sn)
    dma = lambda n: pltpu.SemaphoreType.DMA((n,))
    vmem = pl.BlockSpec(memory_space=pltpu.VMEM)
    hbm = pl.BlockSpec(memory_space=pltpu.HBM)
    d_nodes, gathered = pl.pallas_call(
        functools.partial(main_kernel, nr, nc, relations),
        out_shape=(
            jax.ShapeDtypeStruct((nd, f), BF16),
            jax.ShapeDtypeStruct((2, nr, nz, piece, f), BF16),
        ),
        in_specs=[vmem, vmem, hbm, hbm],
        out_specs=(vmem, vmem),
        scratch_shapes=[
            pltpu.VMEM((nr, tn, width), BF16),
            pltpu.VMEM((tn, f), BF16),
            pltpu.VMEM(weights.shape, BF16),
            pltpu.VMEM((relations * tn, sn), BF16),
            pltpu.VMEM((sn, f), BF16),
            pltpu.VMEM((f, relations * tn), BF16),
            pltpu.VMEM((2, nz, f, nd), F32),
            pltpu.VMEM((nz, f, nd), F32),
            pltpu.VMEM((nz, f, nd), BF16),
            pltpu.VMEM((nz - 1, f, nd), BF16),
            pltpu.VMEM((2, half, f), F32),
            pltpu.VMEM((half, f), F32),
            pltpu.VMEM((nr, plane_rows, f), BF16),
            pltpu.VMEM((nr - 1, plane_rows, f), BF16),
            pltpu.VMEM((nz, piece, f), F32),
            pltpu.VMEM((nz - 1, piece, f), F32),
            dma(2),
            dma(nr - 1), dma(nr - 1),
            dma(nz - 1), dma(nz - 1),
            dma(nz), dma(nz),
            dma(1), dma(1),
            dma(nz - 1), dma(nz - 1),
            dma(1), dma(1),
            dma(nr - 1), dma(nr - 1),
            dma(nz - 1), dma(nz - 1),
            dma(nz - 1), dma(nz - 1),
            dma(nr - 1), dma(nr - 1),
            dma(nr), dma(nr),
        ],
        compiler_params=pltpu.CompilerParams(
            collective_id=0, has_side_effects=True, vmem_limit_bytes=67043328
        ),
    )(out_grad, node_in, weights, dense)
    d_weights = gathered.reshape(relations, f, f).astype(F32)
    return d_nodes, d_weights


def solution(mesh):
    return jax.shard_map(
        functools.partial(body, mesh.shape["row"], mesh.shape["col"]),
        mesh=mesh,
        in_specs=(
            P("col", "row"),
            P(("row", "col"), None),
            P(),
            P(None, "col", "row", None, None, None),
            P(None, "col", "row", None),
            P(None, "col", "row", None),
            P(None, "col", "row"),
        ),
        out_specs=(P(("row", "col"), None), P()),
        check_vma=False,
    )
```

profile of v0, /device:TPU:0, one launch (start us, length us, event | category | flops | bytes accessed | tf_op | source)
XLA Modules:
  0.0 77.7 jit_solution(18213426721582012861)
XLA Ops:
  0.6 1.3 %copy_bitcast_fusion = (s32[3,32]{1,0:T(4,128)}, s32[3,32]{1,0:T(4,128)}) fusion(s32[3,1,1,32]{3,2,1,0:T(1,128)} %param.12, s32[3,1,1,32]{3,2,1,0:T(1,128)} %param.11), kind=kLoop, calls=%fused_computation | loop fusion | bytes 1536
  1.9 5.7 %shard_map.86.a_hbm = bf16[1536,1024]{1,0:T(8,128)(2,1)} custom-call(s32[3,32]{1,0:T(4,128)} %get-tuple-element.7.rows_ref, s32[3,32]{1,0:T(4,128)} %get-tuple-element.6.cols_ref, s32[3]{0:T(128)} %bitcast.10, bf16[3,32,128,128]{3,2,1,0:T(8,128)(2,1)} %bitcast.8), custom_call_target="tpu_custom_call" | custom-call | tf_op jit(solution)/shard_map/pallas_call | solution.py:37
  7.6 65.9 %shard_map.87 = (bf16[128,512]{1,0:T(8,128)(2,1)}, bf16[2,4,4,48,512]{4,3,2,1,0:T(8,128)(2,1)}) custom-call(bf16[512,128]{1,0:T(8,128)(2,1)} %grad_ref.1, bf16[128,512]{1,0:T(8,128)(2,1)} %nodes_ref.1, bf16[3,512,512]{2,1,0:T(8,128)(2,1)} %w_hbm.1, bf16[1536,1024]{1,0:T(8,128)(2,1)} %shard_map.86.a_hbm), custom_call_target="tpu_custom_call" | custom-call | tf_op jit(solution)/shard_map/pallas_call | solution.py:254
  73.5 0.0 copy-start
  73.5 3.5 %convert.1 = f32[3,512,512]{2,1,0:T(8,128)} convert(bf16[3,512,512]{2,1,0:T(8,128)(2,1)} %bitcast.9) | non-fusion elementwise | flops 786432 | bytes 4718592 | tf_op jit(solution)/shard_map/convert_element_type | solution.py:296
  77.1 0.0 copy-done
  77.1 0.7 copy.14
Async XLA Ops:
  73.5 3.6 %copy-start = (bf16[128,512]{1,0:T(8,128)(2,1)S(1)}, bf16[128,512]{1,0:T(8,128)(2,1)}, u32[]{:S(2)}) copy-start(bf16[128,512]{1,0:T(8,128)(2,1)} %get-tuple-element.10) | copy-start | bytes 393220
where the time goes:
time: 78.3 us; the launch traced here: 77.7 us
  Pallas kernels  71.6 us (91%)
  other arithmetic  3.55 us (5%)
  local copies, waits for them, and re-layouts  1.94 us (2%)
    pallas_call x1, Pallas kernels, body(): pl.pallas_call(functools.partial(main_kernel, nr, nc, relations), out_sha...  65.9 us
    pallas_call x1, Pallas kernels, assemble(): pl.pallas_call(assemble_kernel, grid_spec=pltpu.PrefetchScalarGridSpec(nu...  5.72 us
    convert_element_type x1, other arithmetic, body(): d_weights = gathered.reshape(relations, f, f).astype(F32)  3.55 us
    unnamed x4, local copies, waits for them, and re-layouts  1.94 us

commit v1 on v0

--- a/solution.py
+++ b/solution.py
@@ -151,39 +151,110 @@
         return carry
 
     lax.fori_loop(0, nz, combine, 0)
-    n_copies = []
-    for d in range(1, nz):
-        c = remote(ncomb.at[lax.rem(z + d, nz)], ndst.at[d - 1], nzs.at[d - 1], nzr.at[d - 1], z_peer(d))
-        c.start()
-        n_copies.append(c)
+    n_copies = [
+        remote(ncomb.at[lax.rem(z + d, nz)], ndst.at[d - 1], nzs.at[d - 1], nzr.at[d - 1], z_peer(d))
+        for d in range(1, nz)
+    ]
+    for c in n_copies[:-1]:
+        c.start()
 
     for c in f_copies:
         c.wait_recv()
 
     chunk = f // 2
-    for j in range(2 * relations):
-        r, h = j // 2, j % 2
-        y = jnp.dot(
-            a[r * tn : (r + 1) * tn, :],
-            xall[:, h * chunk : (h + 1) * chunk],
-            preferred_element_type=F32,
-        )
-        yt = y.astype(BF16).T
-        at = (j % relations) * chunk
-        dw[j // relations, at : at + chunk, :] = jnp.dot(yt, g[...], preferred_element_type=F32)
-
-    d_core = remote(dw.at[other], dwrecv, ds.at[0], dr.at[0], sibling)
-    d_core.start()
-    d_core.wait_recv()
-    plane_rows = pbuf.shape[1]
-    for k in range(nr):
-        rows = slice(k * plane_rows, (k + 1) * plane_rows)
-        pbuf[k] = (dw[core, rows, :] + dwrecv[rows, :]).astype(BF16)
-    p_copies = []
-    for d in range(1, nr):
-        c = remote(pbuf.at[lax.rem(me_r + d, nr)], precv.at[d - 1], ps.at[d - 1], pr.at[d - 1], row_peer(d))
-        c.start()
-        p_copies.append(c)
+    plane_rows = pbuf.shape[2]
+    piece = zbuf.shape[2]
+    sent = [[] for _ in range(relations)]
+    batches = [[None] * relations for _ in range(5)]
+
+    def launch(stage, r, copies):
+        for c in copies:
+            c.start()
+        batches[stage][r] = copies
+        sent[r].extend(copies)
+
+    def arrived(stage, r):
+        for c in batches[stage][r]:
+            c.wait_recv()
+
+    def terms(r):
+        for h in range(2):
+            y = jnp.dot(
+                a[r * tn : (r + 1) * tn, :],
+                xall[:, h * chunk : (h + 1) * chunk],
+                preferred_element_type=F32,
+            )
+            dw[r, h] = jnp.dot(y.astype(BF16).T, g[...], preferred_element_type=F32)
+        launch(0, r, [remote(dw.at[r, other], dwrecv.at[r], ds.at[r, 0], dr.at[r, 0], sibling)])
+
+    def plane_scatter(r):
+        arrived(0, r)
+        for k in range(nr):
+            rows = slice(k * plane_rows, (k + 1) * plane_rows)
+            pbuf[r, k] = (dw[r, core, rows, :] + dwrecv[r, rows, :]).astype(BF16)
+        launch(1, r, [
+            remote(
+                pbuf.at[r, lax.rem(me_r + d, nr)], precv.at[r, d - 1],
+                ps.at[r, d - 1], pr.at[r, d - 1], row_peer(d),
+            )
+            for d in range(1, nr)
+        ])
+
+    def z_scatter(r):
+        arrived(1, r)
+        for k in range(nz):
+            rows = slice(k * piece, (k + 1) * piece)
+            part = pbuf[r, me_r, rows, :].astype(F32)
+            for d in range(1, nr):
+                part = part + precv[r, d - 1, rows, :].astype(F32)
+            zbuf[r, k] = part.astype(BF16)
+        launch(2, r, [
+            remote(
+                zbuf.at[r, lax.rem(z + d, nz)], zrecv.at[r, d - 1],
+                zs.at[r, d - 1], zr.at[r, d - 1], z_peer(d),
+            )
+            for d in range(1, nz)
+        ])
+
+    def z_gather(r):
+        arrived(2, r)
+        final = zbuf[r, z].astype(F32)
+        for d in range(1, nz):
+            final = final + zrecv[r, d - 1].astype(F32)
+        ag_ref[r, core, me_r, z] = final.astype(BF16)
+        mine = ag_ref.at[r, core, me_r, z]
+        launch(3, r, [remote(mine, mine, azs.at[r, d - 1], azr.at[r, d - 1], z_peer(d)) for d in range(1, nz)])
+
+    last = [[] for _ in range(relations)]
+
+    def plane_gather(r):
+        arrived(3, r)
+        mine = ag_ref.at[r, core, me_r]
+        launch(4, r, [remote(mine, mine, aps.at[r, d - 1], apr.at[r, d - 1], row_peer(d)) for d in range(1, nr)])
+        c = remote(mine, mine, acs.at[r, 0], acr.at[r, 0], sibling)
+        c.start()
+        last[r].append(c)
+
+    def core_gather(r):
+        for d in range(1, nr):
+            batches[4][r][d - 1].wait_recv()
+            slot = ag_ref.at[r, core, lax.rem(me_r + nr - d, nr)]
+            c = remote(slot, slot, acs.at[r, d], acr.at[r, d], sibling)
+            c.start()
+            last[r].append(c)
+
+    terms(0)
+    for r in range(1, relations):
+        terms(r)
+        plane_scatter(r - 1)
+    plane_scatter(relations - 1)
+    stages = (z_scatter, z_gather, plane_gather, core_gather)
+    for t in range(relations + len(stages) - 1):
+        for stage in reversed(range(len(stages))):
+            if 0 <= t - stage < relations:
+                stages[stage](t - stage)
+        if t == relations:
+            n_copies[-1].start()
 
     for c in n_copies:
         c.wait_recv()
@@ -192,49 +263,12 @@
         own = own + ndst[d - 1].astype(F32)
     dn_ref[...] = own.T.astype(BF16)
 
-    for c in p_copies:
-        c.wait_recv()
-    piece = zbuf.shape[1]
-    for k in range(nz):
-        rows = slice(k * piece, (k + 1) * piece)
-        part = pbuf[me_r, rows, :].astype(F32)
-        for d in range(1, nr):
-            part = part + precv[d - 1, rows, :].astype(F32)
-        zbuf[k] = part
-    z_copies = []
-    for d in range(1, nz):
-        c = remote(zbuf.at[lax.rem(z + d, nz)], zrecv.at[d - 1], zs.at[d - 1], zr.at[d - 1], z_peer(d))
-        c.start()
-        z_copies.append(c)
-    for c in z_copies:
-        c.wait_recv()
-    final = zbuf[z]
-    for d in range(1, nz):
-        final = final + zrecv[d - 1]
-    ag_ref[core, me_r, z] = final.astype(BF16)
-
-    tail = []
-    mine = ag_ref.at[core, me_r, z]
-    az = [remote(mine, mine, azs.at[d - 1], azr.at[d - 1], z_peer(d)) for d in range(1, nz)]
-    for c in az:
-        c.start()
-    for c in az:
-        c.wait_recv()
-    mine = ag_ref.at[core, me_r]
-    ap = [remote(mine, mine, aps.at[d - 1], apr.at[d - 1], row_peer(d)) for d in range(1, nr)]
-    for c in ap:
-        c.start()
-    ac = [remote(mine, mine, acs.at[0], acr.at[0], sibling)]
-    ac[0].start()
-    for d in range(1, nr):
-        ap[d - 1].wait_recv()
-        slot = ag_ref.at[core, lax.rem(me_r + nr - d, nr)]
-        c = remote(slot, slot, acs.at[d], acr.at[d], sibling)
-        c.start()
-        ac.append(c)
-    for c in ac:
-        c.wait_recv()
-    for c in g_copies + x_copies + f_copies + [n_core] + n_copies + [d_core] + p_copies + z_copies + az + ap + ac:
+    for r in range(relations):
+        for c in last[r]:
+            c.wait_recv()
+        for c in sent[r] + last[r]:
+            c.wait_send()
+    for c in g_copies + x_copies + f_copies + [n_core] + n_copies:
         c.wait_send()
 
 
@@ -244,18 +278,18 @@
     nd = node_in.shape[0]
     sn = nd * nc
     nz = nc // 2
-    half = relations * f // 2
+    half = f // 2
     plane_rows = half // nr
     piece = plane_rows // nz
     dense = assemble(tile_vals, tile_rows, tile_cols, tile_count, tn, sn)
-    dma = lambda n: pltpu.SemaphoreType.DMA((n,))
+    dma = lambda *n: pltpu.SemaphoreType.DMA(n)
     vmem = pl.BlockSpec(memory_space=pltpu.VMEM)
     hbm = pl.BlockSpec(memory_space=pltpu.HBM)
     d_nodes, gathered = pl.pallas_call(
         functools.partial(main_kernel, nr, nc, relations),
         out_shape=(
             jax.ShapeDtypeStruct((nd, f), BF16),
-            jax.ShapeDtypeStruct((2, nr, nz, piece, f), BF16),
+            jax.ShapeDtypeStruct((relations, 2, nr, nz, piece, f), BF16),
         ),
         in_specs=[vmem, vmem, hbm, hbm],
         out_specs=(vmem, vmem),
@@ -270,24 +304,24 @@
             pltpu.VMEM((nz, f, nd), F32),
             pltpu.VMEM((nz, f, nd), BF16),
             pltpu.VMEM((nz - 1, f, nd), BF16),
-            pltpu.VMEM((2, half, f), F32),
-            pltpu.VMEM((half, f), F32),
-            pltpu.VMEM((nr, plane_rows, f), BF16),
-            pltpu.VMEM((nr - 1, plane_rows, f), BF16),
-            pltpu.VMEM((nz, piece, f), F32),
-            pltpu.VMEM((nz - 1, piece, f), F32),
+            pltpu.VMEM((relations, 2, half, f), F32),
+            pltpu.VMEM((relations, half, f), F32),
+            pltpu.VMEM((relations, nr, plane_rows, f), BF16),
+            pltpu.VMEM((relations, nr - 1, plane_rows, f), BF16),
+            pltpu.VMEM((relations, nz, piece, f), BF16),
+            pltpu.VMEM((relations, nz - 1, piece, f), BF16),
             dma(2),
             dma(nr - 1), dma(nr - 1),
             dma(nz - 1), dma(nz - 1),
             dma(nz), dma(nz),
             dma(1), dma(1),
             dma(nz - 1), dma(nz - 1),
-            dma(1), dma(1),
-            dma(nr - 1), dma(nr - 1),
-            dma(nz - 1), dma(nz - 1),
-            dma(nz - 1), dma(nz - 1),
-            dma(nr - 1), dma(nr - 1),
-            dma(nr), dma(nr),
+            dma(relations, 1), dma(relations, 1),
+            dma(relations, nr - 1), dma(relations, nr - 1),
+            dma(relations, nz - 1), dma(relations, nz - 1),
+            dma(relations, nz - 1), dma(relations, nz - 1),
+            dma(relations, nr - 1), dma(relations, nr - 1),
+            dma(relations, nr), dma(relations, nr),
         ],
         compiler_params=pltpu.CompilerParams(
             collective_id=0, has_side_effects=True, vmem_limit_bytes=67043328

time: 78.3 us -> 69.1 us (0.88)
  Pallas kernels: 71.6 us -> 62.8 us
    pallas_call x1, Pallas kernels: 65.9 us -> 56.9 us  [body(): pl.pallas_call(functools.partial(main_kernel, nr, nc, relations), out_sha...]
where the time goes in v1:
time: 69.1 us; the launch traced here: 68.9 us
  Pallas kernels  62.8 us (91%)
  other arithmetic  3.55 us (5%)
  local copies, waits for them, and re-layouts  1.94 us (3%)
    pallas_call x1, Pallas kernels, body(): pl.pallas_call(functools.partial(main_kernel, nr, nc, relations), out_sha...  56.9 us
    pallas_call x1, Pallas kernels, assemble(): pl.pallas_call(assemble_kernel, grid_spec=pltpu.PrefetchScalarGridSpec(nu...  5.86 us
    convert_element_type x1, other arithmetic, body(): d_weights = gathered.reshape(relations, f, f).astype(F32)  3.55 us
    unnamed x4, local copies, waits for them, and re-layouts  1.94 us

profile of v1, /device:TPU:0, one launch (start us, length us, event | category | flops | bytes accessed | tf_op | source)
XLA Modules:
  0.0 68.9 jit_solution(1741944038982029532)
XLA Ops:
  0.6 1.3 %copy_bitcast_fusion = (s32[3,32]{1,0:T(4,128)}, s32[3,32]{1,0:T(4,128)}) fusion(s32[3,1,1,32]{3,2,1,0:T(1,128)} %param.12, s32[3,1,1,32]{3,2,1,0:T(1,128)} %param.11), kind=kLoop, calls=%fused_computation.1 | loop fusion | bytes 1536
  1.9 5.9 %shard_map.86.a_hbm = bf16[1536,1024]{1,0:T(8,128)(2,1)} custom-call(s32[3,32]{1,0:T(4,128)} %get-tuple-element.7.rows_ref, s32[3,32]{1,0:T(4,128)} %get-tuple-element.6.cols_ref, s32[3]{0:T(128)} %bitcast.10, bf16[3,32,128,128]{3,2,1,0:T(8,128)(2,1)} %bitcast.9), custom_call_target="tpu_custom_call" | custom-call | tf_op jit(solution)/shard_map/pallas_call | solution.py:37
  7.8 56.9 %shard_map.87 = (bf16[128,512]{1,0:T(8,128)(2,1)}, bf16[3,2,4,4,16,512]{5,4,3,2,1,0:T(8,128)(2,1)}) custom-call(bf16[512,128]{1,0:T(8,128)(2,1)} %grad_ref.1, bf16[128,512]{1,0:T(8,128)(2,1)} %nodes_ref.1, bf16[3,512,512]{2,1,0:T(8,128)(2,1)} %w_hbm.1, bf16[1536,1024]{1,0:T(8,128)(2,1)} %shard_map.86.a_hbm), custom_call_target="tpu_custom_call" | custom-call | tf_op jit(solution)/shard_map/pallas_call | solution.py:288
  64.7 0.0 copy-start
  64.7 3.5 %bitcast_convert_fusion = f32[3,512,512]{2,1,0:T(8,128)} fusion(bf16[3,2,4,4,16,512]{5,4,3,2,1,0:T(8,128)(2,1)} %get-tuple-element.5), kind=kLoop, calls=%fused_computation | loop fusion | flops 786432 | bytes 4718592 | tf_op jit(solution)/shard_map/convert_element_type | solution.py:330
  68.3 0.0 copy-done
  68.3 0.7 copy.14
Async XLA Ops:
  64.7 3.6 %copy-start = (bf16[128,512]{1,0:T(8,128)(2,1)S(1)}, bf16[128,512]{1,0:T(8,128)(2,1)}, u32[]{:S(2)}) copy-start(bf16[128,512]{1,0:T(8,128)(2,1)} %get-tuple-element.10) | copy-start | bytes 393220

commit v2 on v1

--- a/solution.py
+++ b/solution.py
@@ -20,8 +20,8 @@
             total[i, j] = jnp.zeros((tile, tile), F32)
 
     def add_tile(slot, carry):
-        i = rows_ref[relation, slot]
-        j = cols_ref[relation, slot]
+        i = rows_ref[relation, 0, 0, slot]
+        j = cols_ref[relation, 0, 0, slot]
         total[i, j] = total[i, j] + tiles_ref[0, slot].astype(F32)
         return carry
 
@@ -46,8 +46,8 @@
         out_shape=jax.ShapeDtypeStruct((relations * targets, sources), BF16),
         compiler_params=pltpu.CompilerParams(vmem_limit_bytes=60 * 2**20),
     )(
-        tile_rows.reshape(relations, cap),
-        tile_cols.reshape(relations, cap),
+        tile_rows,
+        tile_cols,
         tile_count.reshape(relations),
         vals,
     )
@@ -128,9 +128,10 @@
     load_a.wait()
 
     def mix(k, carry):
-        for h in range(2):
-            cols = pl.ds(pl.multiple_of((k * 2 + h) * nd, nd), nd)
-            nsend[h, k] = jnp.dot(pt[...], a[:, cols], preferred_element_type=F32)
+        cols = pl.ds(pl.multiple_of(k * 2 * nd, 2 * nd), 2 * nd)
+        both = jnp.dot(pt[...], a[:, cols], preferred_element_type=F32)
+        nsend[0, k] = both[:, :nd]
+        nsend[1, k] = both[:, nd:]
         return carry
 
     lax.fori_loop(0, nz, mix, 0)
@@ -270,6 +271,28 @@
             c.wait_send()
     for c in g_copies + x_copies + f_copies + [n_core] + n_copies:
         c.wait_send()
+
+
+def widen_kernel(dn_ref, dw_ref, dn_out, dw_out):
+    dn_out[...] = dn_ref[...]
+    dw_out[...] = dw_ref[...].astype(F32)
+
+
+def widen(d_nodes, gathered):
+    relations, f = gathered.shape[0], gathered.shape[1]
+    parts = 2
+    weight = pl.BlockSpec((1, f // parts, f), lambda r, h: (r, h, 0))
+    nodes = pl.BlockSpec(d_nodes.shape, lambda r, h: (0, 0))
+    return pl.pallas_call(
+        widen_kernel,
+        grid=(relations, parts),
+        in_specs=[nodes, weight],
+        out_specs=(nodes, weight),
+        out_shape=(
+            jax.ShapeDtypeStruct(d_nodes.shape, BF16),
+            jax.ShapeDtypeStruct(gathered.shape, F32),
+        ),
+    )(d_nodes, gathered)
 
 
 def body(nr, nc, out_grad, node_in, weights, tile_vals, tile_rows, tile_cols, tile_count):
@@ -327,8 +350,7 @@
             collective_id=0, has_side_effects=True, vmem_limit_bytes=67043328
         ),
     )(out_grad, node_in, weights, dense)
-    d_weights = gathered.reshape(relations, f, f).astype(F32)
-    return d_nodes, d_weights
+    return widen(d_nodes, gathered.reshape(relations, f, f))
 
 
 def solution(mesh):

time: 69.1 us -> 66.9 us (0.968)
  other arithmetic: 3.55 us -> 0 us
  Pallas kernels: 62.8 us -> 65.9 us
  local copies, waits for them, and re-layouts: 1.94 us -> 0 us
    pallas_call x0 -> x1, Pallas kernels: none -> 4.91 us  [widen(): pl.pallas_call(widen_kernel, grid=(relations, parts), in_specs=[nodes, we...]
    convert_element_type x1 -> x0, other arithmetic: 3.55 us -> none  [body(): d_weights = gathered.reshape(relations, f, f).astype(F32)]
    unnamed x4 -> x0, local copies, waits for them, and re-layouts: 1.94 us -> none
    pallas_call x1, Pallas kernels: 56.9 us -> 55.1 us  [body(): pl.pallas_call(functools.partial(main_kernel, nr, nc, relations), out_sha...]
where the time goes in v2:
time: 66.9 us; the launch traced here: 66.6 us
  Pallas kernels  65.9 us (99%)
    pallas_call x1, Pallas kernels, body(): pl.pallas_call(functools.partial(main_kernel, nr, nc, relations), out_sha...  55.1 us
    pallas_call x1, Pallas kernels, assemble(): pl.pallas_call(assemble_kernel, grid_spec=pltpu.PrefetchScalarGridSpec(nu...  5.95 us
    pallas_call x1, Pallas kernels, widen(): pl.pallas_call(widen_kernel, grid=(relations, parts), in_specs=[nodes, we...  4.91 us

profile of v2, /device:TPU:0, one launch (start us, length us, event | category | flops | bytes accessed | tf_op | source)
XLA Modules:
  0.0 66.6 jit_solution(3165460467513688697)
XLA Ops:
  0.6 5.9 %shard_map.86.a_hbm = bf16[1536,1024]{1,0:T(8,128)(2,1)} custom-call(s32[3,1,1,32]{3,2,1,0:T(1,128)} %rows_ref.1, s32[3,1,1,32]{3,2,1,0:T(1,128)} %cols_ref.1, s32[3]{0:T(128)} %bitcast.5, bf16[3,32,128,128]{3,2,1,0:T(8,128)(2,1)} %bitcast.3), custom_call_target="tpu_custom_call" | custom-call | tf_op jit(solution)/shard_map/pallas_call | solution.py:37
  6.6 55.1 %shard_map.87 = (bf16[128,512]{1,0:T(8,128)(2,1)}, bf16[3,2,4,4,16,512]{5,4,3,2,1,0:T(8,128)(2,1)}) custom-call(bf16[512,128]{1,0:T(8,128)(2,1)} %grad_ref.1, bf16[128,512]{1,0:T(8,128)(2,1)} %nodes_ref.1, bf16[3,512,512]{2,1,0:T(8,128)(2,1)} %w_hbm.1, bf16[1536,1024]{1,0:T(8,128)(2,1)} %shard_map.86.a_hbm), custom_call_target="tpu_custom_call" | custom-call | tf_op jit(solution)/shard_map/pallas_call | solution.py:311
  61.7 4.9 %shard_map.88 = (bf16[128,512]{1,0:T(8,128)(2,1)}, f32[3,512,512]{2,1,0:T(8,128)}) custom-call(bf16[128,512]{1,0:T(8,128)(2,1)} %get-tuple-element.4.dn_ref, bf16[3,512,512]{2,1,0:T(8,128)(2,1)} %bitcast.4), custom_call_target="tpu_custom_call" | custom-call | tf_op jit(solution)/shard_map/pallas_call | solution.py:286

commit v3 on v2

--- a/solution.py
+++ b/solution.py
@@ -273,25 +273,48 @@
         c.wait_send()
 
 
-def widen_kernel(dn_ref, dw_ref, dn_out, dw_out):
-    dn_out[...] = dn_ref[...]
-    dw_out[...] = dw_ref[...].astype(F32)
+def widen_kernel(dn_ref, dw_ref, dn_out, dw_out, nodes, narrow, wide, in_sem, out_sem):
+    parts, rows = narrow.shape[0], narrow.shape[1]
+
+    def part(ref, k):
+        return ref.at[k * rows : (k + 1) * rows, :]
+
+    loads = [pltpu.make_async_copy(part(dw_ref, k), narrow.at[k], in_sem.at[k]) for k in range(parts)]
+    stores = [pltpu.make_async_copy(wide.at[k], part(dw_out, k), out_sem.at[k]) for k in range(parts)]
+    loads.append(pltpu.make_async_copy(dn_ref, nodes, in_sem.at[parts]))
+    stores.append(pltpu.make_async_copy(nodes, dn_out, out_sem.at[parts]))
+    for c in loads:
+        c.start()
+    for k in range(parts):
+        loads[k].wait()
+        wide[k] = narrow[k].astype(F32)
+        stores[k].start()
+    loads[parts].wait()
+    stores[parts].start()
+    for c in stores:
+        c.wait()
 
 
 def widen(d_nodes, gathered):
-    relations, f = gathered.shape[0], gathered.shape[1]
-    parts = 2
-    weight = pl.BlockSpec((1, f // parts, f), lambda r, h: (r, h, 0))
-    nodes = pl.BlockSpec(d_nodes.shape, lambda r, h: (0, 0))
+    total, f = gathered.shape
+    parts = 6 if total % 96 == 0 else 1
+    rows = total // parts
+    hbm = pl.BlockSpec(memory_space=pltpu.HBM)
     return pl.pallas_call(
         widen_kernel,
-        grid=(relations, parts),
-        in_specs=[nodes, weight],
-        out_specs=(nodes, weight),
+        in_specs=[hbm, hbm],
+        out_specs=(hbm, hbm),
         out_shape=(
             jax.ShapeDtypeStruct(d_nodes.shape, BF16),
             jax.ShapeDtypeStruct(gathered.shape, F32),
         ),
+        scratch_shapes=[
+            pltpu.VMEM(d_nodes.shape, BF16),
+            pltpu.VMEM((parts, rows, f), BF16),
+            pltpu.VMEM((parts, rows, f), F32),
+            pltpu.SemaphoreType.DMA((parts + 1,)),
+            pltpu.SemaphoreType.DMA((parts + 1,)),
+        ],
     )(d_nodes, gathered)
 
 
@@ -350,7 +373,8 @@
             collective_id=0, has_side_effects=True, vmem_limit_bytes=67043328
         ),
     )(out_grad, node_in, weights, dense)
-    return widen(d_nodes, gathered.reshape(relations, f, f))
+    d_nodes, d_weights = widen(d_nodes, gathered.reshape(relations * f, f))
+    return d_nodes, d_weights.reshape(relations, f, f)
 
 
 def solution(mesh):

time: 66.9 us -> 64.6 us (0.966)
  Pallas kernels: 65.9 us -> 63.6 us
    pallas_call x1, Pallas kernels: 4.91 us -> 2.8 us  [widen(): pl.pallas_call(widen_kernel, in_specs=[hbm, hbm], out_specs=(hbm, hbm), o...]
where the time goes in v3:
time: 64.6 us; the launch traced here: 64.3 us
  Pallas kernels  63.6 us (98%)
    pallas_call x1, Pallas kernels, body(): pl.pallas_call(functools.partial(main_kernel, nr, nc, relations), out_sha...  54.5 us
    pallas_call x1, Pallas kernels, assemble(): pl.pallas_call(assemble_kernel, grid_spec=pltpu.PrefetchScalarGridSpec(nu...  6.33 us
    pallas_call x1, Pallas kernels, widen(): pl.pallas_call(widen_kernel, in_specs=[hbm, hbm], out_specs=(hbm, hbm), o...  2.8 us

profile of v3, /device:TPU:0, one launch (start us, length us, event | category | flops | bytes accessed | tf_op | source)
XLA Modules:
  0.0 64.3 jit_solution(10976164576306861124)
XLA Ops:
  0.6 6.3 %shard_map.86.a_hbm = bf16[1536,1024]{1,0:T(8,128)(2,1)} custom-call(s32[3,1,1,32]{3,2,1,0:T(1,128)} %rows_ref.1, s32[3,1,1,32]{3,2,1,0:T(1,128)} %cols_ref.1, s32[3]{0:T(128)} %bitcast.6, bf16[3,32,128,128]{3,2,1,0:T(8,128)(2,1)} %bitcast.4), custom_call_target="tpu_custom_call" | custom-call | tf_op jit(solution)/shard_map/pallas_call | solution.py:37
  7.0 54.5 %shard_map.87 = (bf16[128,512]{1,0:T(8,128)(2,1)}, bf16[3,2,4,4,16,512]{5,4,3,2,1,0:T(8,128)(2,1)}) custom-call(bf16[512,128]{1,0:T(8,128)(2,1)} %grad_ref.1, bf16[128,512]{1,0:T(8,128)(2,1)} %nodes_ref.1, bf16[3,512,512]{2,1,0:T(8,128)(2,1)} %w_hbm.1, bf16[1536,1024]{1,0:T(8,128)(2,1)} %shard_map.86.a_hbm), custom_call_target="tpu_custom_call" | custom-call | tf_op jit(solution)/shard_map/pallas_call | solution.py:334
  61.5 2.8 %shard_map.88 = (bf16[128,512]{1,0:T(8,128)(2,1)}, f32[1536,512]{1,0:T(8,128)}) custom-call(bf16[128,512]{1,0:T(8,128)(2,1)} %get-tuple-element.6.dn_ref, bf16[1536,512]{1,0:T(8,128)(2,1)} %bitcast.5), custom_call_target="tpu_custom_call" | custom-call | tf_op jit(solution)/shard_map/pallas_call | solution.py:303

commit v4 on v3

--- a/solution.py
+++ b/solution.py
@@ -251,7 +251,7 @@
     plane_scatter(relations - 1)
     stages = (z_scatter, z_gather, plane_gather, core_gather)
     for t in range(relations + len(stages) - 1):
-        for stage in reversed(range(len(stages))):
+        for stage in range(len(stages)):
             if 0 <= t - stage < relations:
                 stages[stage](t - stage)
         if t == relations:

time: 64.6 us -> 60.2 us (0.932)
  Pallas kernels: 63.6 us -> 59.3 us
    pallas_call x1, Pallas kernels: 54.5 us -> 50.7 us  [body(): pl.pallas_call(functools.partial(main_kernel, nr, nc, relations), out_sha...]
where the time goes in v4:
time: 60.2 us; the launch traced here: 59.9 us
  Pallas kernels  59.3 us (99%)
  between operations  0.64 us (1%)
    pallas_call x1, Pallas kernels, body(): pl.pallas_call(functools.partial(main_kernel, nr, nc, relations), out_sha...  50.7 us
    pallas_call x1, Pallas kernels, assemble(): pl.pallas_call(assemble_kernel, grid_spec=pltpu.PrefetchScalarGridSpec(nu...  5.8 us
    pallas_call x1, Pallas kernels, widen(): pl.pallas_call(widen_kernel, in_specs=[hbm, hbm], out_specs=(hbm, hbm), o...  2.8 us

profile of v4, /device:TPU:0, one launch (start us, length us, event | category | flops | bytes accessed | tf_op | source)
XLA Modules:
  0.0 59.9 jit_solution(5539360638715369462)
XLA Ops:
  0.6 5.8 %shard_map.86.a_hbm = bf16[1536,1024]{1,0:T(8,128)(2,1)} custom-call(s32[3,1,1,32]{3,2,1,0:T(1,128)} %rows_ref.1, s32[3,1,1,32]{3,2,1,0:T(1,128)} %cols_ref.1, s32[3]{0:T(128)} %bitcast.6, bf16[3,32,128,128]{3,2,1,0:T(8,128)(2,1)} %bitcast.4), custom_call_target="tpu_custom_call" | custom-call | tf_op jit(solution)/shard_map/pallas_call | solution.py:37
  6.4 50.7 %shard_map.87 = (bf16[128,512]{1,0:T(8,128)(2,1)}, bf16[3,2,4,4,16,512]{5,4,3,2,1,0:T(8,128)(2,1)}) custom-call(bf16[512,128]{1,0:T(8,128)(2,1)} %grad_ref.1, bf16[128,512]{1,0:T(8,128)(2,1)} %nodes_ref.1, bf16[3,512,512]{2,1,0:T(8,128)(2,1)} %w_hbm.1, bf16[1536,1024]{1,0:T(8,128)(2,1)} %shard_map.86.a_hbm), custom_call_target="tpu_custom_call" | custom-call | tf_op jit(solution)/shard_map/pallas_call | solution.py:334
  57.1 2.8 %shard_map.88 = (bf16[128,512]{1,0:T(8,128)(2,1)}, f32[1536,512]{1,0:T(8,128)}) custom-call(bf16[128,512]{1,0:T(8,128)(2,1)} %get-tuple-element.6.dn_ref, bf16[1536,512]{1,0:T(8,128)(2,1)} %bitcast.5), custom_call_target="tpu_custom_call" | custom-call | tf_op jit(solution)/shard_map/pallas_call | solution.py:303
